TPU v7x, 512 devices: a 8x2x16 block of a 8x8x16 slice. The times are simulated.
512 devices in a mesh: prompt: 2 (over y), seq: 16 (over z), blk: 8 (over x), cfg: 2 (over core).
Axes of the slice: x: 8, y: 2, z: 16, core: 2. Of those that a mesh axis runs over, the one named last changes fastest.
The devices are a block of a 8x8x16 slice.
Arguments:
- queries: bfloat16 [2, 12288, 4096], P('cfg', ('prompt', 'blk', 'seq')), parts along dimension 1, may hold values from -5 to 5
- key_states: bfloat16 [2, 12288, 4096], P('cfg', ('prompt', 'blk', 'seq')), parts along dimension 1, may hold values from -5 to 5
- value_states: bfloat16 [2, 12288, 4096], P('cfg', ('prompt', 'blk', 'seq')), parts along dimension 1, may hold values from -6 to 6
- noisy_latents: float32 [12288, 64], P(('prompt', 'blk', 'seq')), parts along dimension 0, may hold values from -6 to 6
- patch_order: int32 [12288], P(('prompt', 'blk', 'seq')), parts along dimension 0, may hold values from 0 to 6143, as said below
- head_weight: bfloat16 [4096, 64], replicated, may hold values from -0.75 to 0.75
- latent_std: float32 [16], replicated, may hold values from 0.1 to 1.9
- latent_mean: float32 [16], replicated, may hold values from -3 to 3
- conv_weight: bfloat16 [3, 3, 3, 16, 384], replicated, may hold values from -0.3125 to 0.3125
- conv_bias: float32 [384], replicated, may hold values from -2 to 2
Outputs:
- features: bfloat16 [16, 64, 48, 384], P(('prompt', 'cfg'), 'seq', 'blk'), parts along dimension 0
There are 2 independent parts, one for each index of `prompt`. A program takes and returns all parts, laid end to end along the dimension named above; an argument that names none is the same for every part. Nothing has to cross between parts.
Inputs may be any that keep to these rules, and one draw needn't show every extreme that they name: A permutation of 0 to 6143 that keeps every aligned block of 48 tokens within itself: patch_order[t] // 48 == t // 48.
All inputs are finite; a program needn't handle non-finite values.
Results may differ from a plain program's by a relative error of at most 0.012.
Values may be sent and summed in bfloat16 or wider, within the bound.
A program may use at most 128 MiB of HBM per device.

v0:
```python
import math
import jax
import jax.numpy as jnp
from jax import lax
from jax.sharding import PartitionSpec as P

HDIM = 128
ZCH = 16
COLS_DEV = 3
GUIDE = 5.0
NOISE_LEVEL = 0.5


def split_up(array, dim, devices):
    lengths = array.shape
    pieces = array.reshape(*lengths[:dim], devices, lengths[dim] // devices, *lengths[dim + 1 :])
    return jnp.moveaxis(pieces, dim, 0)


def sum_at_owner(array, axis, dim):
    devices = lax.axis_size(axis)
    pieces = lax.all_to_all(split_up(array, dim, devices), axis, 0, 0, tiled=True)
    return jnp.sum(pieces.astype(jnp.float32), axis=0)


def partner(array, axis, apart):
    return lax.ppermute(array, axis, [(i, i ^ 1 << apart) for i in range(lax.axis_size(axis))])


def padded(array, sides, width):
    for axis, dim in sides:
        devices, length = (lax.axis_size(axis), array.shape[dim])
        up = [(i, (i + 1) % devices) for i in range(devices - 1)]
        down = [(j, i) for i, j in up]
        last = lax.slice_in_dim(array, length - width, length, axis=dim)
        first = lax.slice_in_dim(array, 0, width, axis=dim)
        before = lax.ppermute(last, axis, up)
        after = lax.ppermute(first, axis, down)
        array = jnp.concatenate([before, array, after], axis=dim)
    return array


def fold_keys(carry, piece, grouped, block):
    keys_piece, values_piece = piece
    heads = grouped.shape[1]
    count = keys_piece.shape[0] // block
    key_blocks = keys_piece.reshape(count, block, heads, HDIM)
    value_blocks = values_piece.reshape(count, block, heads, HDIM)
    scale = 1.0 / math.sqrt(HDIM)

    def one_block(state, pair):
        top, total, acc = state
        key_block, value_block = pair
        scores = (
            jnp.einsum("qhd,khd->hqk", grouped, key_block, preferred_element_type=jnp.float32)
            * scale
        )
        new_top = jnp.maximum(top, jnp.max(scores, axis=2))
        expo = jnp.exp(scores - new_top[:, :, None])
        factor = jnp.exp(top - new_top)
        total = total * factor + jnp.sum(expo, axis=2)
        weights = expo.astype(jnp.bfloat16)
        update = jnp.einsum(
            "hqk,khd->qhd", weights, value_block, preferred_element_type=jnp.float32
        )
        acc = acc * factor.T[:, :, None] + update
        return ((new_top, total, acc), None)

    state, unused = lax.scan(one_block, carry, (key_blocks, value_blocks))
    return state


def start_for(rows, heads):
    return (
        jnp.full((heads, rows), -1e30, jnp.float32),
        jnp.zeros((heads, rows), jnp.float32),
        jnp.zeros((rows, heads, HDIM), jnp.float32),
    )


def finish(state):
    top, total, acc = state
    rows = acc.shape[0]
    return (acc / total.T[:, :, None]).astype(jnp.bfloat16).reshape(rows, acc.shape[1] * HDIM)


def local(
    queries,
    key_states,
    value_states,
    noisy_latents,
    patch_order,
    head_weight,
    latent_std,
    latent_mean,
    conv_weight,
    conv_bias,
):
    seq_count = lax.axis_size("seq")
    blk_count = lax.axis_size("blk")
    seq_index = lax.axis_index("seq")
    blk_index = lax.axis_index("blk")
    cfg_index = lax.axis_index("cfg")
    tok_rows = queries.shape[1]
    own_query = queries[0]
    own_keys = key_states[0]
    own_values = value_states[0]
    local_query, local_keys, local_values = (
        lax.all_to_all(own_query, "seq", split_axis=1, concat_axis=0, tiled=True),
        lax.all_to_all(own_keys, "seq", split_axis=1, concat_axis=0, tiled=True),
        lax.all_to_all(own_values, "seq", split_axis=1, concat_axis=0, tiled=True),
    )
    frame_rows = local_query.shape[0]
    heads = local_query.shape[1] // HDIM
    grouped = local_query.reshape(frame_rows, heads, HDIM)
    state = fold_keys(
        start_for(frame_rows, heads),
        (
            lax.all_gather(local_keys, "blk", axis=0, tiled=True),
            lax.all_gather(local_values, "blk", axis=0, tiled=True),
        ),
        grouped,
        frame_rows,
    )
    attended = finish(state)
    weight_rows = lax.dynamic_slice_in_dim(
        head_weight, seq_index * attended.shape[1], attended.shape[1], 0
    )
    velocity = sum_at_owner(
        jnp.dot(attended, weight_rows, preferred_element_type=jnp.float32).astype(jnp.bfloat16),
        "seq",
        0,
    )
    other = partner(velocity, "cfg", 0)
    is_cond = cfg_index == 0
    cond = jnp.where(is_cond, velocity, other)
    uncond = jnp.where(is_cond, other, velocity)
    guided = uncond + GUIDE * (cond - uncond)
    denoised = noisy_latents - NOISE_LEVEL * guided
    pixels = (
        denoised * jnp.tile(latent_std, 4)[None, :] + jnp.tile(latent_mean, 4)[None, :]
    ).astype(jnp.bfloat16)
    block_start = (blk_index * seq_count + seq_index) * tok_rows
    local_slot = patch_order - block_start
    selector = (jnp.arange(tok_rows, dtype=jnp.int32)[:, None] == local_slot[None, :]).astype(
        jnp.bfloat16
    )
    placed = jnp.dot(selector, pixels, preferred_element_type=jnp.float32).astype(jnp.bfloat16)
    grid_cols = COLS_DEV * blk_count
    strip_rows = tok_rows // grid_cols
    strip = placed.reshape(1, strip_rows, grid_cols * placed.shape[1])
    received = lax.all_to_all(strip, "blk", split_axis=2, concat_axis=0, tiled=True)
    frame_count = received.shape[0]
    tile = (
        received.reshape(frame_count, strip_rows, COLS_DEV, 2, 2, ZCH)
        .transpose(0, 1, 3, 2, 4, 5)
        .reshape(frame_count, 2 * strip_rows, 2 * COLS_DEV, ZCH)
    )
    half = frame_count // 2
    leading = jnp.zeros((2,) + tile.shape[1:], jnp.bfloat16)
    timeline = jnp.concatenate([leading, tile], axis=0)
    window = lax.dynamic_slice_in_dim(timeline, cfg_index * half, half + 2, 0)
    framed = padded(window, (("seq", 1), ("blk", 2)), 1)
    tile_rows = 2 * strip_rows
    tile_cols = 2 * COLS_DEV
    columns = []
    for step_t in range(3):
        for step_y in range(3):
            for step_x in range(3):
                columns.append(
                    framed[
                        step_t : step_t + half,
                        step_y : step_y + tile_rows,
                        step_x : step_x + tile_cols,
                        :,
                    ]
                )
    stacked = jnp.concatenate(columns, axis=3).reshape(half * tile_rows * tile_cols, 27 * ZCH)
    kernel = conv_weight.reshape(27 * ZCH, conv_weight.shape[4])
    output = jnp.dot(stacked, kernel, preferred_element_type=jnp.float32) + conv_bias[None, :]
    return output.reshape(half, tile_rows, tile_cols, conv_weight.shape[4]).astype(jnp.bfloat16)


def solution(mesh):
    in_specs = (
        P("cfg", ("prompt", "blk", "seq"), None),
        P("cfg", ("prompt", "blk", "seq"), None),
        P("cfg", ("prompt", "blk", "seq"), None),
        P(("prompt", "blk", "seq"), None),
        P(("prompt", "blk", "seq")),
        P(),
        P(),
        P(),
        P(),
        P(),
    )
    out_specs = P(("prompt", "cfg"), "seq", "blk", None)
    return jax.shard_map(local, mesh=mesh, in_specs=in_specs, out_specs=out_specs, check_vma=False)
```

profile of v0, /device:TPU:66, one launch (start us, length us, event | category | flops | bytes accessed | tf_op | source)
XLA Modules:
  0.0 339.0 jit_solution(12205130973058300356)
XLA Ops:
  6.6 1.2 copy.77
  7.8 67.3 %all_to_all.74 = bf16[48,16,256]{2,0,1:T(8,128)(2,1)} all-to-all(bf16[48,16,256]{2,0,1:T(8,128)(2,1)S(1)} %copy.52), channel_id=1, replica_groups=mesh['prompt'=2,'seq'=16,'blk'=8,'cfg'=2] {'seq'}, dimensions={1} | all-to-all | bytes 786432 | tf_op jit(solution)/shard_map/all_to_all | solution.py:110
  75.3 1.1 copy.79
  76.5 29.7 %all_to_all.75 = bf16[48,16,256]{2,0,1:T(8,128)(2,1)} all-to-all(bf16[48,16,256]{2,0,1:T(8,128)(2,1)S(1)} %copy.55), channel_id=1, replica_groups=mesh['prompt'=2,'seq'=16,'blk'=8,'cfg'=2] {'seq'}, dimensions={1} | all-to-all | bytes 786432 | tf_op jit(solution)/shard_map/all_to_all | solution.py:111
  106.3 0.9 copy.54
  107.2 6.2 %all-to-all-start.1 = ((bf16[48,16,256]{2,0,1:T(8,128)(2,1)}), bf16[48,16,256]{2,0,1:T(8,128)(2,1)S(1)}, u32[]{:S(2)}, u32[]{:S(2)}) async-start(bf16[48,16,256]{2,0,1:T(8,128)(2,1)} %copy.54), calls=%async_computation.1 | async-start | bytes 786432 | tf_op jit(solution)/shard_map/all_to_all | solution.py:109
  113.4 23.1 %all-to-all-done.1 = bf16[48,16,256]{2,0,1:T(8,128)(2,1)S(1)} async-done(((bf16[48,16,256]{2,0,1:T(8,128)(2,1)}), bf16[48,16,256]{2,0,1:T(8,128)(2,1)S(1)}, u32[]{:S(2)}, u32[]{:S(2)}) %all-to-all-start.1) | async-done | bytes 393248 | tf_op jit(solution)/shard_map/all_to_all | solution.py:109
  136.7 5.5 %reshape.65 = bf16[8,768,2,128]{3,2,1,0:T(2,128)(2,1)} reshape(bf16[6144,256]{1,0:T(8,128)(2,1)} %all-gather.3.cloned.1.call-done) | data formatting | bytes 6291456 | tf_op jit(solution)/shard_map/reshape | solution.py:47
  142.2 32.6 %all-gather.5.cloned.1.call-done = bf16[6144,256]{1,0:T(8,128)(2,1)} async-done(((bf16[768,256]{1,0:T(8,128)(2,1)}), bf16[6144,256]{1,0:T(8,128)(2,1)}) %all-gather.5.cloned.1.call-update) | async-done | bytes 3145744 | tf_op jit(solution)/shard_map/all_gather | solution.py:120
  174.8 5.5 %reshape.66 = bf16[8,768,2,128]{3,2,1,0:T(2,128)(2,1)} reshape(bf16[6144,256]{1,0:T(8,128)(2,1)} %all-gather.5.cloned.1.call-done) | data formatting | bytes 6291456 | tf_op jit(solution)/shard_map/reshape | solution.py:48
  180.3 77.1 %while.15 = (s32[]{:T(128)}, f32[2,768]{1,0:T(2,128)S(1)}, f32[2,768]{1,0:T(2,128)S(1)}, f32[768,2,128]{0,2,1:T(8,128)S(1)}, bf16[8,768,2,128]{3,2,1,0:T(2,128)(...) while((s32[]{:T(128)}, f32[2,768]{1,0:T(2,128)S(1)}, ...), condition=%wide.region_3.4_spmd.clone, body=%wide.region_0.3_spmd.clone.sunk | while | flops 614016000 | bytes 38240392 | solution.py:69
  180.3 1.7 constant_dynamic-slice_fusion.3
  182.0 2.9 bitcast_reduce_fusion.2
  185.4 3.6 %fusion.54 = f32[768,2,128]{0,2,1:T(8,128)S(1)} fusion(f32[2,768,768]{2,1,0:T(8,128)} %get-tuple-element.214, f32[2,768]{1,0:T(2,128)S(1)} %get-tuple-element.236, f32[768,2,128]{0,2,1:T(8,128)S(1)} %get-tuple-element.229, bf16[1,768,2,128]{1,3,2,0:T(8,128)(2,1)S(1)} %copy.87, f32[768,2]{0,1:T(2,128)S(1)} %get-tuple-element.216, pred[]{:T(512)S(6)} %compare.4), kind=kOutput, calls=%fused_computation.9.clone.1 | convolution fusion | flops 306118656 | bytes 6696961 | tf_op jit(solution)/shard_map/while/body/eval_jaxpr/hqk,khd->qhd/dot_general | solution.py:63
  189.1 0.8 fusion.52
  190.0 1.7 constant_dynamic-slice_fusion.3
  191.6 2.9 bitcast_reduce_fusion.2
  195.0 3.6 %fusion.54 = f32[768,2,128]{0,2,1:T(8,128)S(1)} fusion(f32[2,768,768]{2,1,0:T(8,128)} %get-tuple-element.214, f32[2,768]{1,0:T(2,128)S(1)} %get-tuple-element.236, f32[768,2,128]{0,2,1:T(8,128)S(1)} %get-tuple-element.229, bf16[1,768,2,128]{1,3,2,0:T(8,128)(2,1)S(1)} %copy.87, f32[768,2]{0,1:T(2,128)S(1)} %get-tuple-element.216, pred[]{:T(512)S(6)} %compare.4), kind=kOutput, calls=%fused_computation.9.clone.1 | convolution fusion | flops 306118656 | bytes 6696961 | tf_op jit(solution)/shard_map/while/body/eval_jaxpr/hqk,khd->qhd/dot_general | solution.py:63
  198.8 0.8 fusion.52
  199.6 1.7 constant_dynamic-slice_fusion.3
  201.3 2.9 bitcast_reduce_fusion.2
  204.6 3.6 %fusion.54 = f32[768,2,128]{0,2,1:T(8,128)S(1)} fusion(f32[2,768,768]{2,1,0:T(8,128)} %get-tuple-element.214, f32[2,768]{1,0:T(2,128)S(1)} %get-tuple-element.236, f32[768,2,128]{0,2,1:T(8,128)S(1)} %get-tuple-element.229, bf16[1,768,2,128]{1,3,2,0:T(8,128)(2,1)S(1)} %copy.87, f32[768,2]{0,1:T(2,128)S(1)} %get-tuple-element.216, pred[]{:T(512)S(6)} %compare.4), kind=kOutput, calls=%fused_computation.9.clone.1 | convolution fusion | flops 306118656 | bytes 6696961 | tf_op jit(solution)/shard_map/while/body/eval_jaxpr/hqk,khd->qhd/dot_general | solution.py:63
  208.4 0.8 fusion.52
  209.2 1.7 constant_dynamic-slice_fusion.3
  210.9 2.9 bitcast_reduce_fusion.2
  214.3 3.6 %fusion.54 = f32[768,2,128]{0,2,1:T(8,128)S(1)} fusion(f32[2,768,768]{2,1,0:T(8,128)} %get-tuple-element.214, f32[2,768]{1,0:T(2,128)S(1)} %get-tuple-element.236, f32[768,2,128]{0,2,1:T(8,128)S(1)} %get-tuple-element.229, bf16[1,768,2,128]{1,3,2,0:T(8,128)(2,1)S(1)} %copy.87, f32[768,2]{0,1:T(2,128)S(1)} %get-tuple-element.216, pred[]{:T(512)S(6)} %compare.4), kind=kOutput, calls=%fused_computation.9.clone.1 | convolution fusion | flops 306118656 | bytes 6696961 | tf_op jit(solution)/shard_map/while/body/eval_jaxpr/hqk,khd->qhd/dot_general | solution.py:63
  218.0 0.8 fusion.52
  218.9 1.7 constant_dynamic-slice_fusion.3
  220.5 2.9 bitcast_reduce_fusion.2
  223.9 3.6 %fusion.54 = f32[768,2,128]{0,2,1:T(8,128)S(1)} fusion(f32[2,768,768]{2,1,0:T(8,128)} %get-tuple-element.214, f32[2,768]{1,0:T(2,128)S(1)} %get-tuple-element.236, f32[768,2,128]{0,2,1:T(8,128)S(1)} %get-tuple-element.229, bf16[1,768,2,128]{1,3,2,0:T(8,128)(2,1)S(1)} %copy.87, f32[768,2]{0,1:T(2,128)S(1)} %get-tuple-element.216, pred[]{:T(512)S(6)} %compare.4), kind=kOutput, calls=%fused_computation.9.clone.1 | convolution fusion | flops 306118656 | bytes 6696961 | tf_op jit(solution)/shard_map/while/body/eval_jaxpr/hqk,khd->qhd/dot_general | solution.py:63
  227.7 0.8 fusion.52
  228.5 1.7 constant_dynamic-slice_fusion.3
  230.2 2.9 bitcast_reduce_fusion.2
  233.6 3.6 %fusion.54 = f32[768,2,128]{0,2,1:T(8,128)S(1)} fusion(f32[2,768,768]{2,1,0:T(8,128)} %get-tuple-element.214, f32[2,768]{1,0:T(2,128)S(1)} %get-tuple-element.236, f32[768,2,128]{0,2,1:T(8,128)S(1)} %get-tuple-element.229, bf16[1,768,2,128]{1,3,2,0:T(8,128)(2,1)S(1)} %copy.87, f32[768,2]{0,1:T(2,128)S(1)} %get-tuple-element.216, pred[]{:T(512)S(6)} %compare.4), kind=kOutput, calls=%fused_computation.9.clone.1 | convolution fusion | flops 306118656 | bytes 6696961 | tf_op jit(solution)/shard_map/while/body/eval_jaxpr/hqk,khd->qhd/dot_general | solution.py:63
  237.3 0.8 fusion.52
  238.1 1.7 constant_dynamic-slice_fusion.3
  239.8 2.9 bitcast_reduce_fusion.2
  243.2 3.6 %fusion.54 = f32[768,2,128]{0,2,1:T(8,128)S(1)} fusion(f32[2,768,768]{2,1,0:T(8,128)} %get-tuple-element.214, f32[2,768]{1,0:T(2,128)S(1)} %get-tuple-element.236, f32[768,2,128]{0,2,1:T(8,128)S(1)} %get-tuple-element.229, bf16[1,768,2,128]{1,3,2,0:T(8,128)(2,1)S(1)} %copy.87, f32[768,2]{0,1:T(2,128)S(1)} %get-tuple-element.216, pred[]{:T(512)S(6)} %compare.4), kind=kOutput, calls=%fused_computation.9.clone.1 | convolution fusion | flops 306118656 | bytes 6696961 | tf_op jit(solution)/shard_map/while/body/eval_jaxpr/hqk,khd->qhd/dot_general | solution.py:63
  246.9 0.8 fusion.52
  247.8 1.7 constant_dynamic-slice_fusion.3
  249.4 2.9 bitcast_reduce_fusion.2
  252.8 3.6 %fusion.54 = f32[768,2,128]{0,2,1:T(8,128)S(1)} fusion(f32[2,768,768]{2,1,0:T(8,128)} %get-tuple-element.214, f32[2,768]{1,0:T(2,128)S(1)} %get-tuple-element.236, f32[768,2,128]{0,2,1:T(8,128)S(1)} %get-tuple-element.229, bf16[1,768,2,128]{1,3,2,0:T(8,128)(2,1)S(1)} %copy.87, f32[768,2]{0,1:T(2,128)S(1)} %get-tuple-element.216, pred[]{:T(512)S(6)} %compare.4), kind=kOutput, calls=%fused_computation.9.clone.1 | convolution fusion | flops 306118656 | bytes 6696961 | tf_op jit(solution)/shard_map/while/body/eval_jaxpr/hqk,khd->qhd/dot_general | solution.py:63
  256.6 0.8 fusion.52
  257.9 0.8 reshape.67
  258.7 13.1 %all-to-all-start.3 = ((bf16[16,2,1536]{2,1,0:T(2,128)(2,1)}), bf16[16,2,1536]{2,1,0:T(2,128)(2,1)S(1)}, u32[]{:S(2)}, u32[]{:S(2)}) async-start(bf16[16,2,1536]{2,1,0:T(2,128)(2,1)} %reshape.67), calls=%async_computation.3 | async-start | bytes 196608 | tf_op jit(solution)/shard_map/all_to_all | solution.py:22
  271.8 12.9 %all-to-all-done.3 = bf16[16,2,1536]{2,1,0:T(2,128)(2,1)S(1)} async-done(((bf16[16,2,1536]{2,1,0:T(2,128)(2,1)}), bf16[16,2,1536]{2,1,0:T(2,128)(2,1)S(1)}, u32[]{:S(2)}, u32[]{:S(2)}) %all-to-all-start.3) | async-done | bytes 98336 | tf_op jit(solution)/shard_map/all_to_all | solution.py:22
  285.0 2.1 collective-permute-start
  287.5 0.7 collective-permute-done
  288.5 0.7 copy.63
  289.1 0.5 broadcast.58
  289.6 8.8 %reduce = bf16[1536,2]{1,0:T(8,128)(2,1)S(1)} reduce(bf16[1536,1,2]{2,1,0:T(2,128)(2,1)S(1)} %bitcast.77, bf16[]{:T(256)} %broadcast.58), dimensions={1}, to_apply=%bitcast.53.reduce_sub_computation | reduce | bytes 12290
  298.5 1.1 reshape.69
  299.6 5.7 %all-to-all-start.4 = ((bf16[8,2,192]{2,1,0:T(2,128)(2,1)}), bf16[8,2,192]{2,1,0:T(2,128)(2,1)S(1)}, u32[]{:S(2)}, u32[]{:S(2)}) async-start(bf16[8,2,192]{2,1,0:T(2,128)(2,1)} %reshape.69), calls=%async_computation.4 | async-start | bytes 16384 | tf_op jit(solution)/shard_map/all_to_all | solution.py:152
  305.3 6.3 %all-to-all-done.4 = bf16[8,2,192]{2,1,0:T(2,128)(2,1)S(1)} async-done(((bf16[8,2,192]{2,1,0:T(2,128)(2,1)}), bf16[8,2,192]{2,1,0:T(2,128)(2,1)S(1)}, u32[]{:S(2)}, u32[]{:S(2)}) %all-to-all-start.4) | async-done | bytes 6176 | tf_op jit(solution)/shard_map/all_to_all | solution.py:152
  311.6 0.9 reshape.70
  312.5 0.5 copy.64
  313.3 2.9 collective-permute-start.1
  316.2 1.3 collective-permute-start.2
  317.7 4.1 %collective-permute-done.2 = bf16[6,1,6,16]{3,0,2,1:T(8,128)(2,1)S(1)} collective-permute-done((bf16[6,1,6,16]{3,0,2,1:T(8,128)(2,1)S(1)}, bf16[6,1,6,16]{3,0,2,1:T(8,128)(2,1)S(1)}, u32[]{:S(2)}, u32[]{:S(2)}) %collective-permute-start.2) | collective-permute-done | bytes 1184 | tf_op jit(solution)/shard_map/ppermute | solution.py:38
  321.8 2.5 collective-permute-start.3
  324.3 3.4 %collective-permute-start.4 = (bf16[6,6,1,16]{3,0,2,1:T(8,128)(2,1)S(1)}, bf16[6,6,1,16]{3,0,2,1:T(8,128)(2,1)S(1)}, u32[]{:S(2)}, u32[]{:S(2)}) collective-permute-start(bf16[6,6,1,16]{3,0,2,1:T(8,128)(2,1)S(1)} %get-tuple-element.137), channel_id=1, source_target_pairs={{2,0},{4,2},{6,4},{8,6},{10,8},{12,10},{14,12},{3,1},{5,3},{7,5},{... | collective-permute-start | bytes 3464 | tf_op jit(solution)/shard_map/ppermute | solution.py:38
  327.8 2.1 collective-permute-done.4
  330.1 1.0 concatenate.48
  331.5 0.7 copy.67
  (107 shorter events, 7.6 us)
Async XLA Ops:
  6.5 251.0 %copy-start = (bf16[4096,64]{0,1:T(8,128)(2,1)S(1)}, bf16[4096,64]{0,1:T(8,128)(2,1)}, u32[]{:S(2)}) copy-start(bf16[4096,64]{0,1:T(8,128)(2,1)} %param.17) | copy-start | bytes 1572868
  6.6 99.6 %copy-start.2 = (bf16[1,48,4096]{2,1,0:T(8,128)(2,1)S(1)}, bf16[1,48,4096]{2,1,0:T(8,128)(2,1)}, u32[]{:S(2)}) copy-start(bf16[1,48,4096]{2,1,0:T(8,128)(2,1)} %param.12) | copy-start | bytes 1179652
  6.6 130.1 %all-gather.3.cloned.1.call-start = ((), (), s32[]{:S(2)}) async-start(), calls=%async_computation.5 | async-start | bytes 3538944 | tf_op jit(solution)/shard_map/all_gather | solution.py:119
  75.2 99.6 %all-gather.5.cloned.1.call-start = ((), (), s32[]{:S(2)}) async-start(), calls=%async_computation.6 | async-start | bytes 3538944 | tf_op jit(solution)/shard_map/all_gather | solution.py:120
  107.2 29.3 %all-to-all-start.1 = ((bf16[48,16,256]{2,0,1:T(8,128)(2,1)}), bf16[48,16,256]{2,0,1:T(8,128)(2,1)S(1)}, u32[]{:S(2)}, u32[]{:S(2)}) async-start(bf16[48,16,256]{2,0,1:T(8,128)(2,1)} %copy.54), calls=%async_computation.1 | async-start | bytes 786432 | tf_op jit(solution)/shard_map/all_to_all | solution.py:109
  180.3 106.9 %copy-start.8 = (s32[48]{0:T(128)S(1)}, s32[48]{0:T(128)}, u32[]{:S(2)}) copy-start(s32[48]{0:T(128)} %param.16) | copy-start | bytes 580
  180.3 106.9 %copy-start.4 = (f32[48,64]{1,0:T(8,128)S(1)}, f32[48,64]{1,0:T(8,128)}, u32[]{:S(2)}) copy-start(f32[48,64]{1,0:T(8,128)} %param.15) | copy-start | bytes 36868
  180.3 107.0 %copy-start.6 = (f32[16]{0:T(128)S(1)}, f32[16]{0:T(128)}, u32[]{:S(2)}) copy-start(f32[16]{0:T(128)} %param.19) | copy-start | bytes 196
  180.3 107.1 %copy-start.7 = (f32[16]{0:T(128)S(1)}, f32[16]{0:T(128)}, u32[]{:S(2)}) copy-start(f32[16]{0:T(128)} %param.18) | copy-start | bytes 196
  185.4 3.8 %copy-start.1 = (f32[2,768,768]{2,1,0:T(8,128)S(1)}, f32[2,768,768]{2,1,0:T(8,128)}, u32[]{:S(2)}) copy-start(f32[2,768,768]{2,1,0:T(8,128)} %get-tuple-element.214) | copy-start | bytes 14155780 | tf_op jit(solution)/shard_map/while
  195.0 3.8 %copy-start.1 = (f32[2,768,768]{2,1,0:T(8,128)S(1)}, f32[2,768,768]{2,1,0:T(8,128)}, u32[]{:S(2)}) copy-start(f32[2,768,768]{2,1,0:T(8,128)} %get-tuple-element.214) | copy-start | bytes 14155780 | tf_op jit(solution)/shard_map/while
  204.6 3.8 %copy-start.1 = (f32[2,768,768]{2,1,0:T(8,128)S(1)}, f32[2,768,768]{2,1,0:T(8,128)}, u32[]{:S(2)}) copy-start(f32[2,768,768]{2,1,0:T(8,128)} %get-tuple-element.214) | copy-start | bytes 14155780 | tf_op jit(solution)/shard_map/while
  214.3 3.8 %copy-start.1 = (f32[2,768,768]{2,1,0:T(8,128)S(1)}, f32[2,768,768]{2,1,0:T(8,128)}, u32[]{:S(2)}) copy-start(f32[2,768,768]{2,1,0:T(8,128)} %get-tuple-element.214) | copy-start | bytes 14155780 | tf_op jit(solution)/shard_map/while
  223.9 3.8 %copy-start.1 = (f32[2,768,768]{2,1,0:T(8,128)S(1)}, f32[2,768,768]{2,1,0:T(8,128)}, u32[]{:S(2)}) copy-start(f32[2,768,768]{2,1,0:T(8,128)} %get-tuple-element.214) | copy-start | bytes 14155780 | tf_op jit(solution)/shard_map/while
  233.5 3.8 %copy-start.1 = (f32[2,768,768]{2,1,0:T(8,128)S(1)}, f32[2,768,768]{2,1,0:T(8,128)}, u32[]{:S(2)}) copy-start(f32[2,768,768]{2,1,0:T(8,128)} %get-tuple-element.214) | copy-start | bytes 14155780 | tf_op jit(solution)/shard_map/while
  243.2 3.8 %copy-start.1 = (f32[2,768,768]{2,1,0:T(8,128)S(1)}, f32[2,768,768]{2,1,0:T(8,128)}, u32[]{:S(2)}) copy-start(f32[2,768,768]{2,1,0:T(8,128)} %get-tuple-element.214) | copy-start | bytes 14155780 | tf_op jit(solution)/shard_map/while
  252.8 3.8 %copy-start.1 = (f32[2,768,768]{2,1,0:T(8,128)S(1)}, f32[2,768,768]{2,1,0:T(8,128)}, u32[]{:S(2)}) copy-start(f32[2,768,768]{2,1,0:T(8,128)} %get-tuple-element.214) | copy-start | bytes 14155780 | tf_op jit(solution)/shard_map/while
  257.5 73.7 %copy-start.3 = (bf16[3,3,3,16,384]{4,3,2,1,0:T(8,128)(2,1)S(1)}, bf16[3,3,3,16,384]{4,3,2,1,0:T(8,128)(2,1)}, u32[]{:S(2)}) copy-start(bf16[3,3,3,16,384]{4,3,2,1,0:T(8,128)(2,1)} %param.20) | copy-start | bytes 995332
  257.5 73.7 %copy-start.5 = (f32[384]{0:T(512)S(1)}, f32[384]{0:T(512)}, u32[]{:S(2)}) copy-start(f32[384]{0:T(512)} %param.21) | copy-start | bytes 4612
  258.7 26.0 %all-to-all-start.3 = ((bf16[16,2,1536]{2,1,0:T(2,128)(2,1)}), bf16[16,2,1536]{2,1,0:T(2,128)(2,1)S(1)}, u32[]{:S(2)}, u32[]{:S(2)}) async-start(bf16[16,2,1536]{2,1,0:T(2,128)(2,1)} %reshape.67), calls=%async_computation.3 | async-start | bytes 196608 | tf_op jit(solution)/shard_map/all_to_all | solution.py:22
  285.0 3.1 collective-permute-start
  299.6 12.0 %all-to-all-start.4 = ((bf16[8,2,192]{2,1,0:T(2,128)(2,1)}), bf16[8,2,192]{2,1,0:T(2,128)(2,1)S(1)}, u32[]{:S(2)}, u32[]{:S(2)}) async-start(bf16[8,2,192]{2,1,0:T(2,128)(2,1)} %reshape.69), calls=%async_computation.4 | async-start | bytes 16384 | tf_op jit(solution)/shard_map/all_to_all | solution.py:152
  313.3 4.4 %collective-permute-start.1 = (bf16[6,1,6,16]{3,0,2,1:T(8,128)(2,1)S(1)}, bf16[6,1,6,16]{3,0,2,1:T(8,128)(2,1)S(1)}, u32[]{:S(2)}, u32[]{:S(2)}) collective-permute-start(bf16[6,1,6,16]{3,0,2,1:T(8,128)(2,1)S(1)} %get-tuple-element.151), channel_id=1, source_target_pairs={{0,16},{16,32},{32,48},{48,64},{64,80},{80,96},{96,112},{112,128},... | collective-permute-start | bytes 3464 | tf_op jit(solution)/shard_map/ppermute | solution.py:37
  316.2 5.6 %collective-permute-start.2 = (bf16[6,1,6,16]{3,0,2,1:T(8,128)(2,1)S(1)}, bf16[6,1,6,16]{3,0,2,1:T(8,128)(2,1)S(1)}, u32[]{:S(2)}, u32[]{:S(2)}) collective-permute-start(bf16[6,1,6,16]{3,0,2,1:T(8,128)(2,1)S(1)} %get-tuple-element.152), channel_id=1, source_target_pairs={{16,0},{32,16},{48,32},{64,48},{80,64},{96,80},{112,96},{128,112},... | collective-permute-start | bytes 3464 | tf_op jit(solution)/shard_map/ppermute | solution.py:38
  321.8 6.0 %collective-permute-start.3 = (bf16[6,6,1,16]{3,0,2,1:T(8,128)(2,1)S(1)}, bf16[6,6,1,16]{3,0,2,1:T(8,128)(2,1)S(1)}, u32[]{:S(2)}, u32[]{:S(2)}) collective-permute-start(bf16[6,6,1,16]{3,0,2,1:T(8,128)(2,1)S(1)} %get-tuple-element.138), channel_id=1, source_target_pairs={{0,2},{2,4},{4,6},{6,8},{8,10},{10,12},{12,14},{1,3},{3,5},{5,7},{... | collective-permute-start | bytes 3464 | tf_op jit(solution)/shard_map/ppermute | solution.py:37
  324.3 5.6 %collective-permute-start.4 = (bf16[6,6,1,16]{3,0,2,1:T(8,128)(2,1)S(1)}, bf16[6,6,1,16]{3,0,2,1:T(8,128)(2,1)S(1)}, u32[]{:S(2)}, u32[]{:S(2)}) collective-permute-start(bf16[6,6,1,16]{3,0,2,1:T(8,128)(2,1)S(1)} %get-tuple-element.137), channel_id=1, source_target_pairs={{2,0},{4,2},{6,4},{8,6},{10,8},{12,10},{14,12},{3,1},{5,3},{7,5},{... | collective-permute-start | bytes 3464 | tf_op jit(solution)/shard_map/ppermute | solution.py:38
Sparse Core Ops, SparseCore 0:
  75.3 46.9 all-gather.2
  124.4 50.3 all-gather.4
where the time goes:
time: 340 us; the launch traced here: 339 us
  blocking collectives  97 us (29%)
  waiting for transfers between devices  81.9 us (24%)
  matrix products  53 us (16%)
  local copies, waits for them, and re-layouts  39.8 us (12%)
  starting transfers between devices  37.3 us (11%)
  other arithmetic  15.6 us (5%)
  between operations  13.8 us (4%)
    all_to_all x1, blocking collectives, local(): lax.all_to_all(own_keys, 'seq', split_axis=1, concat_axis=0, tiled=True)  67.3 us
    all_gather x1, waiting for transfers between devices, local(): lax.all_gather(local_values, 'blk', axis=0, tiled=True)  32.6 us
    all_to_all x1, blocking collectives, local(): lax.all_to_all(own_values, 'seq', split_axis=1, concat_axis=0, tiled=True)  29.7 us
    dot_general x8, matrix products, one_block(): jnp.einsum('hqk,khd->qhd', weights, value_block, preferred_element_type=j...  29 us
    dot_general x8, matrix products, one_block(): jnp.einsum('qhd,khd->hqk', grouped, key_block, preferred_element_type=jnp...  23.3 us
    all_to_all x1, waiting for transfers between devices, local(): lax.all_to_all(own_query, 'seq', split_axis=1, concat_axis=0, tiled=True)  23.1 us
    dynamic_slice x16, local copies, waits for them, and re-layouts, fold_keys(): state, unused = lax.scan(one_block, carry, (key_blocks, value_blocks))  16.8 us
    all_to_all x1, starting transfers between devices, sum_at_owner(): lax.all_to_all(split_up(array, dim, devices), axis, 0, 0, tiled=True)  13.1 us
  transfers between devices with their start and end apart: 10, of which 7 were waited for; matrix products, arithmetic and copies ran while one was open for 2% of the time, Pallas kernels for 0%

commit v1 on v0

--- a/solution.py
+++ b/solution.py
@@ -117,7 +117,12 @@
         start_for(frame_rows, heads),
         (
             lax.all_gather(local_keys, "blk", axis=0, tiled=True),
-            lax.all_gather(local_values, "blk", axis=0, tiled=True),
+            jnp.concatenate(
+                jax.lax.all_to_all(
+                    jnp.stack([local_values] * jax.lax.axis_size("blk")), "blk", 0, 0
+                ),
+                axis=0,
+            ),
         ),
         grouped,
         frame_rows,

time: 340 us -> 395 us (1.16)
  waiting for transfers between devices: 81.9 us -> 180 us
  blocking collectives: 97 us -> 0 us
  starting transfers between devices: 37.3 us -> 98.2 us
  local copies, waits for them, and re-layouts: 39.8 us -> 31 us
    all_to_all x2 -> x0, blocking collectives: 97 us -> none  [the longest x1 67.3 us: local(): lax.all_to_all(own_keys, 'seq', split_axis=1, concat_axis=0, tiled=True)]
    all_gather x1, waiting for transfers between devices: 0.02 us -> 78.4 us  [local(): lax.all_gather(local_keys, 'blk', axis=0, tiled=True)]
    all_to_all x0 -> x3, starting transfers between devices: none -> 57.5 us  [the longest x1 43.7 us: local(): lax.all_to_all(own_values, 'seq', split_axis=1, concat_axis=0, tiled=True)]
    all_to_all x0 -> x3, waiting for transfers between devices: none -> 52.3 us  [the longest x1 22.6 us: local(): lax.all_to_all(own_keys, 'seq', split_axis=1, concat_axis=0, tiled=True)]
    all_gather x1 -> x0, waiting for transfers between devices: 32.6 us -> none  [local(): lax.all_gather(local_values, 'blk', axis=0, tiled=True)]
    dynamic_slice x16 -> x8, local copies, waits for them, and re-layouts: 16.8 us -> 10.2 us  [fold_keys(): state, unused = lax.scan(one_block, carry, (key_blocks, value_blocks))]
    reshape x1 -> x0, local copies, waits for them, and re-layouts: 5.5 us -> none  [fold_keys(): value_blocks = values_piece.reshape(count, block, heads, HDIM)]
  transfers between devices with their start and end apart: 10 -> 12, of which waited for: 7 -> 10; matrix products, arithmetic and copies ran while one was open for 2% -> 3% of each run, Pallas kernels for 0% -> 0%
where the time goes in v1:
time: 395 us; the launch traced here: 394 us
  waiting for transfers between devices  180 us (46%)
  starting transfers between devices  98.2 us (25%)
  matrix products  54.8 us (14%)
  local copies, waits for them, and re-layouts  31 us (8%)
  other arithmetic  15.6 us (4%)
  between operations  13.8 us (3%)
    all_gather x1, waiting for transfers between devices, local(): lax.all_gather(local_keys, 'blk', axis=0, tiled=True)  78.4 us
    all_to_all x1, starting transfers between devices, local(): lax.all_to_all(own_values, 'seq', split_axis=1, concat_axis=0, tiled=True)  43.7 us
    dot_general x8, matrix products, one_block(): jnp.einsum('hqk,khd->qhd', weights, value_block, preferred_element_type=j...  30 us
    dot_general x8, matrix products, one_block(): jnp.einsum('qhd,khd->hqk', grouped, key_block, preferred_element_type=jnp...  24.2 us
    all_to_all x1, waiting for transfers between devices, local(): lax.all_to_all(own_keys, 'seq', split_axis=1, concat_axis=0, tiled=True)  22.6 us
    all_to_all x1, waiting for transfers between devices, local(): lax.all_to_all(own_query, 'seq', split_axis=1, concat_axis=0, tiled=True)  22.4 us
    all_to_all x1, waiting for transfers between devices, local(): lax.all_to_all(own_values, 'seq', split_axis=1, concat_axis=0, tiled=True)  21.8 us
    all_to_all x1, waiting for transfers between devices, sum_at_owner(): lax.all_to_all(split_up(array, dim, devices), axis, 0, 0, tiled=True)  13.3 us
  transfers between devices with their start and end apart: 12, of which 10 were waited for; matrix products, arithmetic and copies ran while one was open for 3% of the time, Pallas kernels for 0%

profile of v1, /device:TPU:66, one launch (start us, length us, event | category | flops | bytes accessed | tf_op | source)
XLA Modules:
  0.0 393.8 jit_solution(7235096622142404765)
XLA Ops:
  6.6 1.2 copy.72
  7.7 0.9 copy.52
  8.6 43.7 %all-to-all-start.2 = ((bf16[48,16,256]{2,0,1:T(8,128)(2,1)}), bf16[48,16,256]{2,0,1:T(8,128)(2,1)S(1)}, u32[]{:S(2)}, u32[]{:S(2)}) async-start(bf16[48,16,256]{2,0,1:T(8,128)(2,1)} %copy.52), calls=%async_computation.2 | async-start | bytes 786432 | tf_op jit(solution)/shard_map/all_to_all | solution.py:111
  52.3 1.1 copy.70
  53.3 0.9 copy.49
  54.2 21.8 %all-to-all-done.2 = bf16[48,16,256]{2,0,1:T(8,128)(2,1)S(1)} async-done(((bf16[48,16,256]{2,0,1:T(8,128)(2,1)}), bf16[48,16,256]{2,0,1:T(8,128)(2,1)S(1)}, u32[]{:S(2)}, u32[]{:S(2)}) %all-to-all-start.2) | async-done | bytes 393248 | tf_op jit(solution)/shard_map/all_to_all | solution.py:111
  76.0 6.1 %all-to-all-start = ((bf16[48,16,256]{2,0,1:T(8,128)(2,1)}), bf16[48,16,256]{2,0,1:T(8,128)(2,1)S(1)}, u32[]{:S(2)}, u32[]{:S(2)}) async-start(bf16[48,16,256]{2,0,1:T(8,128)(2,1)} %copy.49), calls=%async_computation | async-start | bytes 786432 | tf_op jit(solution)/shard_map/all_to_all | solution.py:110
  82.2 0.9 copy.51
  83.1 22.6 %all-to-all-done = bf16[48,16,256]{2,0,1:T(8,128)(2,1)S(1)} async-done(((bf16[48,16,256]{2,0,1:T(8,128)(2,1)}), bf16[48,16,256]{2,0,1:T(8,128)(2,1)S(1)}, u32[]{:S(2)}, u32[]{:S(2)}) %all-to-all-start) | async-done | bytes 393248 | tf_op jit(solution)/shard_map/all_to_all | solution.py:110
  105.7 6.2 %all-to-all-start.1 = ((bf16[48,16,256]{2,0,1:T(8,128)(2,1)}), bf16[48,16,256]{2,0,1:T(8,128)(2,1)S(1)}, u32[]{:S(2)}, u32[]{:S(2)}) async-start(bf16[48,16,256]{2,0,1:T(8,128)(2,1)} %copy.51), calls=%async_computation.1 | async-start | bytes 786432 | tf_op jit(solution)/shard_map/all_to_all | solution.py:109
  112.7 22.4 %all-to-all-done.1 = bf16[48,16,256]{2,0,1:T(8,128)(2,1)S(1)} async-done(((bf16[48,16,256]{2,0,1:T(8,128)(2,1)}), bf16[48,16,256]{2,0,1:T(8,128)(2,1)S(1)}, u32[]{:S(2)}, u32[]{:S(2)}) %all-to-all-start.1) | async-done | bytes 393248 | tf_op jit(solution)/shard_map/all_to_all | solution.py:109
  135.1 1.9 stack.5
  136.9 7.7 %all-to-all-start.3 = ((bf16[8,768,256]{1,2,0:T(8,128)(2,1)}), bf16[8,768,256]{1,2,0:T(8,128)(2,1)}, u32[]{:S(2)}, u32[]{:S(2)}) async-start(bf16[8,768,256]{1,2,0:T(8,128)(2,1)} %stack.5), calls=%async_computation.3 | async-start | bytes 6291456 | tf_op jit(solution)/shard_map/all_to_all | solution.py:121
  144.8 78.4 %all-gather.2.cloned.1.call-done = bf16[6144,256]{1,0:T(8,128)(2,1)} async-done(((bf16[768,256]{1,0:T(8,128)(2,1)}), bf16[6144,256]{1,0:T(8,128)(2,1)}) %all-gather.2.cloned.1.call-update) | async-done | bytes 3145744 | tf_op jit(solution)/shard_map/all_gather | solution.py:119
  223.2 5.5 %reshape.64 = bf16[8,768,2,128]{3,2,1,0:T(2,128)(2,1)} reshape(bf16[6144,256]{1,0:T(8,128)(2,1)} %all-gather.2.cloned.1.call-done) | data formatting | bytes 6291456 | tf_op jit(solution)/shard_map/reshape | solution.py:47
  228.7 7.9 %all-to-all-done.3 = bf16[8,768,256]{1,2,0:T(8,128)(2,1)} async-done(((bf16[8,768,256]{1,2,0:T(8,128)(2,1)}), bf16[8,768,256]{1,2,0:T(8,128)(2,1)}, u32[]{:S(2)}, u32[]{:S(2)}) %all-to-all-start.3) | async-done | bytes 3145760 | tf_op jit(solution)/shard_map/all_to_all | solution.py:121
  236.6 72.0 %while.15 = (s32[]{:T(128)}, f32[2,768]{1,0:T(2,128)S(1)}, f32[2,768]{1,0:T(2,128)S(1)}, f32[768,2,128]{0,2,1:T(8,128)S(1)}, bf16[8,768,2,128]{3,2,1,0:T(2,128)(...) while((s32[]{:T(128)}, f32[2,768]{1,0:T(2,128)S(1)}, ...), condition=%wide.region_3.4_spmd.clone, body=%wide.region_0.3_spmd.clone.sunk | while | flops 614016000 | bytes 36668040 | solution.py:69
  236.6 1.3 constant_dynamic-slice_fusion.2
  237.9 3.0 bitcast_reduce_fusion.2
  241.0 3.8 fusion.56
  244.8 0.8 fusion.54
  245.7 1.3 constant_dynamic-slice_fusion.2
  246.9 3.0 bitcast_reduce_fusion.2
  250.0 3.7 fusion.56
  253.8 0.8 fusion.54
  254.7 1.3 constant_dynamic-slice_fusion.2
  255.9 3.0 bitcast_reduce_fusion.2
  259.0 3.8 fusion.56
  262.8 0.8 fusion.54
  263.7 1.3 constant_dynamic-slice_fusion.2
  264.9 3.0 bitcast_reduce_fusion.2
  268.0 3.8 fusion.56
  271.8 0.8 fusion.54
  272.7 1.3 constant_dynamic-slice_fusion.2
  273.9 3.0 bitcast_reduce_fusion.2
  277.0 3.7 fusion.56
  280.8 0.8 fusion.54
  281.6 1.3 constant_dynamic-slice_fusion.2
  282.9 3.0 bitcast_reduce_fusion.2
  286.0 3.8 fusion.56
  289.8 0.8 fusion.54
  290.6 1.3 constant_dynamic-slice_fusion.2
  291.9 3.0 bitcast_reduce_fusion.2
  295.0 3.8 fusion.56
  299.6 1.3 constant_dynamic-slice_fusion.2
  300.9 3.0 bitcast_reduce_fusion.2
  304.0 3.7 fusion.56
  307.8 0.8 fusion.54
  309.1 0.8 reshape.65
  309.9 13.1 %all-to-all-start.4 = ((bf16[16,2,1536]{2,1,0:T(2,128)(2,1)}), bf16[16,2,1536]{2,1,0:T(2,128)(2,1)S(1)}, u32[]{:S(2)}, u32[]{:S(2)}) async-start(bf16[16,2,1536]{2,1,0:T(2,128)(2,1)} %reshape.65), calls=%async_computation.4 | async-start | bytes 196608 | tf_op jit(solution)/shard_map/all_to_all | solution.py:22
  323.0 13.3 %all-to-all-done.4 = bf16[16,2,1536]{2,1,0:T(2,128)(2,1)S(1)} async-done(((bf16[16,2,1536]{2,1,0:T(2,128)(2,1)}), bf16[16,2,1536]{2,1,0:T(2,128)(2,1)S(1)}, u32[]{:S(2)}, u32[]{:S(2)}) %all-to-all-start.4) | async-done | bytes 98336 | tf_op jit(solution)/shard_map/all_to_all | solution.py:22
  336.6 2.1 collective-permute-start
  341.2 8.8 %reduce = bf16[1536,2]{1,0:T(8,128)(2,1)S(1)} reduce(bf16[1536,1,2]{2,1,0:T(2,128)(2,1)S(1)} %bitcast.78, bf16[]{:T(256)} %broadcast.59), dimensions={1}, to_apply=%bitcast.54.reduce_sub_computation | reduce | bytes 12290
  350.0 1.1 reshape.67
  351.1 8.8 %all-to-all-start.5 = ((bf16[8,2,192]{2,1,0:T(2,128)(2,1)}), bf16[8,2,192]{2,1,0:T(2,128)(2,1)S(1)}, u32[]{:S(2)}, u32[]{:S(2)}) async-start(bf16[8,2,192]{2,1,0:T(2,128)(2,1)} %reshape.67), calls=%async_computation.5 | async-start | bytes 16384 | tf_op jit(solution)/shard_map/all_to_all | solution.py:157
  360.0 6.3 %all-to-all-done.5 = bf16[8,2,192]{2,1,0:T(2,128)(2,1)S(1)} async-done(((bf16[8,2,192]{2,1,0:T(2,128)(2,1)}), bf16[8,2,192]{2,1,0:T(2,128)(2,1)S(1)}, u32[]{:S(2)}, u32[]{:S(2)}) %all-to-all-start.5) | async-done | bytes 6176 | tf_op jit(solution)/shard_map/all_to_all | solution.py:157
  366.3 0.9 reshape.68
  367.9 3.1 collective-permute-start.1
  371.1 1.3 collective-permute-start.2
  372.5 4.1 %collective-permute-done.2 = bf16[6,1,6,16]{3,0,2,1:T(8,128)(2,1)S(1)} collective-permute-done((bf16[6,1,6,16]{3,0,2,1:T(8,128)(2,1)S(1)}, bf16[6,1,6,16]{3,0,2,1:T(8,128)(2,1)S(1)}, u32[]{:S(2)}, u32[]{:S(2)}) %collective-permute-start.2) | collective-permute-done | bytes 1184 | tf_op jit(solution)/shard_map/ppermute | solution.py:38
  376.7 2.5 collective-permute-start.3
  379.2 3.4 collective-permute-start.4
  382.7 2.1 collective-permute-done.4
  385.0 1.0 concatenate.48
  (103 shorter events, 8.0 us)
Async XLA Ops:
  6.5 302.2 %copy-start = (bf16[4096,64]{0,1:T(8,128)(2,1)S(1)}, bf16[4096,64]{0,1:T(8,128)(2,1)}, u32[]{:S(2)}) copy-start(bf16[4096,64]{0,1:T(8,128)(2,1)} %param.17) | copy-start | bytes 1572868
  6.6 75.6 %copy-start.3 = (bf16[1,48,4096]{2,1,0:T(8,128)(2,1)S(1)}, bf16[1,48,4096]{2,1,0:T(8,128)(2,1)}, u32[]{:S(2)}) copy-start(bf16[1,48,4096]{2,1,0:T(8,128)(2,1)} %param.12) | copy-start | bytes 1179652
  8.6 67.4 %all-to-all-start.2 = ((bf16[48,16,256]{2,0,1:T(8,128)(2,1)}), bf16[48,16,256]{2,0,1:T(8,128)(2,1)S(1)}, u32[]{:S(2)}, u32[]{:S(2)}) async-start(bf16[48,16,256]{2,0,1:T(8,128)(2,1)} %copy.52), calls=%async_computation.2 | async-start | bytes 786432 | tf_op jit(solution)/shard_map/all_to_all | solution.py:111
  76.0 29.8 %all-to-all-start = ((bf16[48,16,256]{2,0,1:T(8,128)(2,1)}), bf16[48,16,256]{2,0,1:T(8,128)(2,1)S(1)}, u32[]{:S(2)}, u32[]{:S(2)}) async-start(bf16[48,16,256]{2,0,1:T(8,128)(2,1)} %copy.49), calls=%async_computation | async-start | bytes 786432 | tf_op jit(solution)/shard_map/all_to_all | solution.py:110
  105.7 6.4 %copy-start.2 = (bf16[48,16,256]{2,0,1:T(8,128)(2,1)}, bf16[48,16,256]{2,0,1:T(8,128)(2,1)S(1)}, u32[]{:S(2)}) copy-start(bf16[48,16,256]{2,0,1:T(8,128)(2,1)S(1)} %all-to-all-done) | copy-start | bytes 1179652
  105.7 29.3 %all-to-all-start.1 = ((bf16[48,16,256]{2,0,1:T(8,128)(2,1)}), bf16[48,16,256]{2,0,1:T(8,128)(2,1)S(1)}, u32[]{:S(2)}, u32[]{:S(2)}) async-start(bf16[48,16,256]{2,0,1:T(8,128)(2,1)} %copy.51), calls=%async_computation.1 | async-start | bytes 786432 | tf_op jit(solution)/shard_map/all_to_all | solution.py:109
  111.9 111.3 %all-gather.2.cloned.1.call-start = ((), (), s32[]{:S(2)}) async-start(), calls=%async_computation.6 | async-start | bytes 3538944 | tf_op jit(solution)/shard_map/all_gather | solution.py:119
  136.9 99.7 %all-to-all-start.3 = ((bf16[8,768,256]{1,2,0:T(8,128)(2,1)}), bf16[8,768,256]{1,2,0:T(8,128)(2,1)}, u32[]{:S(2)}, u32[]{:S(2)}) async-start(bf16[8,768,256]{1,2,0:T(8,128)(2,1)} %stack.5), calls=%async_computation.3 | async-start | bytes 6291456 | tf_op jit(solution)/shard_map/all_to_all | solution.py:121
  236.6 102.1 %copy-start.9 = (s32[48]{0:T(128)S(1)}, s32[48]{0:T(128)}, u32[]{:S(2)}) copy-start(s32[48]{0:T(128)} %param.16) | copy-start | bytes 580
  236.6 102.2 %copy-start.5 = (f32[48,64]{1,0:T(8,128)S(1)}, f32[48,64]{1,0:T(8,128)}, u32[]{:S(2)}) copy-start(f32[48,64]{1,0:T(8,128)} %param.15) | copy-start | bytes 36868
  236.6 102.2 %copy-start.7 = (f32[16]{0:T(128)S(1)}, f32[16]{0:T(128)}, u32[]{:S(2)}) copy-start(f32[16]{0:T(128)} %param.19) | copy-start | bytes 196
  236.6 102.3 %copy-start.8 = (f32[16]{0:T(128)S(1)}, f32[16]{0:T(128)}, u32[]{:S(2)}) copy-start(f32[16]{0:T(128)} %param.18) | copy-start | bytes 196
  241.0 3.9 copy-start.1
  250.0 3.9 copy-start.1
  259.0 3.9 copy-start.1
  268.0 3.9 copy-start.1
  277.0 3.9 copy-start.1
  285.9 3.9 copy-start.1
  294.9 3.9 copy-start.1
  303.9 3.9 copy-start.1
  308.7 77.4 %copy-start.4 = (bf16[3,3,3,16,384]{4,3,2,1,0:T(8,128)(2,1)S(1)}, bf16[3,3,3,16,384]{4,3,2,1,0:T(8,128)(2,1)}, u32[]{:S(2)}) copy-start(bf16[3,3,3,16,384]{4,3,2,1,0:T(8,128)(2,1)} %param.20) | copy-start | bytes 995332
  308.7 77.4 %copy-start.6 = (f32[384]{0:T(512)S(1)}, f32[384]{0:T(512)}, u32[]{:S(2)}) copy-start(f32[384]{0:T(512)} %param.21) | copy-start | bytes 4612
  309.9 26.4 %all-to-all-start.4 = ((bf16[16,2,1536]{2,1,0:T(2,128)(2,1)}), bf16[16,2,1536]{2,1,0:T(2,128)(2,1)S(1)}, u32[]{:S(2)}, u32[]{:S(2)}) async-start(bf16[16,2,1536]{2,1,0:T(2,128)(2,1)} %reshape.65), calls=%async_computation.4 | async-start | bytes 196608 | tf_op jit(solution)/shard_map/all_to_all | solution.py:22
  336.6 3.1 collective-permute-start
  351.1 15.1 %all-to-all-start.5 = ((bf16[8,2,192]{2,1,0:T(2,128)(2,1)}), bf16[8,2,192]{2,1,0:T(2,128)(2,1)S(1)}, u32[]{:S(2)}, u32[]{:S(2)}) async-start(bf16[8,2,192]{2,1,0:T(2,128)(2,1)} %reshape.67), calls=%async_computation.5 | async-start | bytes 16384 | tf_op jit(solution)/shard_map/all_to_all | solution.py:157
  367.9 4.6 %collective-permute-start.1 = (bf16[6,1,6,16]{3,0,2,1:T(8,128)(2,1)S(1)}, bf16[6,1,6,16]{3,0,2,1:T(8,128)(2,1)S(1)}, u32[]{:S(2)}, u32[]{:S(2)}) collective-permute-start(bf16[6,1,6,16]{3,0,2,1:T(8,128)(2,1)S(1)} %get-tuple-element.149), channel_id=1, source_target_pairs={{0,16},{16,32},{32,48},{48,64},{64,80},{80,96},{96,112},{112,128},... | collective-permute-start | bytes 3464 | tf_op jit(solution)/shard_map/ppermute | solution.py:37
  371.1 5.6 %collective-permute-start.2 = (bf16[6,1,6,16]{3,0,2,1:T(8,128)(2,1)S(1)}, bf16[6,1,6,16]{3,0,2,1:T(8,128)(2,1)S(1)}, u32[]{:S(2)}, u32[]{:S(2)}) collective-permute-start(bf16[6,1,6,16]{3,0,2,1:T(8,128)(2,1)S(1)} %get-tuple-element.150), channel_id=1, source_target_pairs={{16,0},{32,16},{48,32},{64,48},{80,64},{96,80},{112,96},{128,112},... | collective-permute-start | bytes 3464 | tf_op jit(solution)/shard_map/ppermute | solution.py:38
  376.7 6.0 %collective-permute-start.3 = (bf16[6,6,1,16]{3,0,2,1:T(8,128)(2,1)S(1)}, bf16[6,6,1,16]{3,0,2,1:T(8,128)(2,1)S(1)}, u32[]{:S(2)}, u32[]{:S(2)}) collective-permute-start(bf16[6,6,1,16]{3,0,2,1:T(8,128)(2,1)S(1)} %get-tuple-element.136), channel_id=1, source_target_pairs={{0,2},{2,4},{4,6},{6,8},{8,10},{10,12},{12,14},{1,3},{3,5},{5,7},{... | collective-permute-start | bytes 3464 | tf_op jit(solution)/shard_map/ppermute | solution.py:37
  379.2 5.6 %collective-permute-start.4 = (bf16[6,6,1,16]{3,0,2,1:T(8,128)(2,1)S(1)}, bf16[6,6,1,16]{3,0,2,1:T(8,128)(2,1)S(1)}, u32[]{:S(2)}, u32[]{:S(2)}) collective-permute-start(bf16[6,6,1,16]{3,0,2,1:T(8,128)(2,1)S(1)} %get-tuple-element.135), channel_id=1, source_target_pairs={{2,0},{4,2},{6,4},{8,6},{10,8},{12,10},{14,12},{3,1},{5,3},{7,5},{... | collective-permute-start | bytes 3464 | tf_op jit(solution)/shard_map/ppermute | solution.py:38
Sparse Core Ops, SparseCore 0:
  114.9 108.3 all-gather.1
